TPU v7x, 32 devices: a 4x4x1 block of a 4x4x8 slice. The times are simulated.
32 devices in a mesh: prob: 1 (over z), feat: 32 (over y, x, core).
Axes of the slice: x: 4, y: 4, z: 1, core: 2. Of those that a mesh axis runs over, the one named last changes fastest.
The devices are a block of a 4x4x8 slice.
Arguments:
- design: bfloat16 [16384, 32768], P('prob', 'feat')
- targets: float32 [16384, 100], P('prob')
- weights_init: float32 [32768, 100], P(('prob', 'feat'))
- step_sizes: float32 [32768], P(('prob', 'feat'))
Outputs:
- output 1: float32 [32768, 100], P(('prob', 'feat'))
- output 2: float32 [16384, 100], P('prob')
All inputs are finite; a program needn't handle non-finite values.
Results may differ from a plain program's by a relative error of at most 0.001.
Values are sent between devices in bfloat16 or wider.
A program may use at most 768 MiB of HBM per device.

v0:
```python
import jax
import jax.numpy as jnp
from jax import lax
from jax.sharding import PartitionSpec as P, NamedSharding

SWEEPS = 6
RIDGE_COEF = 1.0
MIX_WEIGHT = 0.75


def solution(mesh):
    def local_solve(design, targets, weights, step_sizes):
        samples = design.shape[0]
        ridge_val = RIDGE_COEF / samples
        step_col = step_sizes[:, None]
        partial = jnp.dot(design, weights.astype(jnp.bfloat16), preferred_element_type=jnp.float32)
        residual = targets - lax.psum(partial, 'feat')
        for _ in range(SWEEPS):
            gradient = lax.dot_general(design, residual.astype(jnp.bfloat16), (((0,), (0,)), ((), ())), preferred_element_type=jnp.float32) / samples
            update = step_col * (gradient - ridge_val * weights)
            weights = weights + MIX_WEIGHT * update
            contrib = jnp.dot(design, update.astype(jnp.bfloat16), preferred_element_type=jnp.float32)
            residual = residual - MIX_WEIGHT * lax.psum(contrib, 'feat')
        return weights, residual

    return jax.shard_map(
        local_solve,
        mesh=mesh,
        in_specs=(P('prob', 'feat'), P('prob', None), P(('prob', 'feat'), None), P(('prob', 'feat'))),
        out_specs=(P(('prob', 'feat'), None), P('prob', None)),
        check_vma=False,
    )
```

profile of v0, /device:TPU:97, one launch (start us, length us, event | category | flops | bytes accessed | tf_op | source)
XLA Modules:
  0.0 1032.2 jit_solution(18186412245484127799)
XLA Ops:
  7.2 0.1 all-reduce.8.cloned.1.call-start
  7.2 24.0 %fusion.90 = f32[16384,100]{0,1:T(8,128)} fusion(bf16[16384,1024]{1,0:T(8,128)(2,1)} %param.4, f32[1024,100]{0,1:T(8,128)} %param.6), kind=kOutput, calls=%fused_computation.60 | convolution fusion | flops 3355545600 | bytes 40517632 | tf_op jit(solution)/shard_map/dot_general | solution.py:16
  31.2 0.1 all-reduce.8.cloned.1.call-update
  31.3 0.0 copy-start
  31.3 0.0 copy-start.1
  31.3 0.4 all-reduce.10.cloned.1.call-start
  31.7 109.9 %all-reduce.8.cloned.1.call-done = f32[16384,100]{0,1:T(8,128)} async-done(((f32[16384,100]{0,1:T(8,128)}), f32[16384,100]{0,1:T(8,128)}) %all-reduce.8.cloned.1.call-update) | async-done | bytes 6553616 | tf_op jit(solution)/shard_map/psum | solution.py:17
  141.5 8.5 sub.39
  150.0 0.0 copy-done
  150.1 0.0 copy-done.1
  150.1 15.1 %fusion.81 = f32[1024,100]{0,1:T(8,128)S(1)} fusion(bf16[16384,1024]{1,0:T(8,128)(2,1)} %param.4, f32[16384,100]{0,1:T(8,128)} %sub.39, f32[1024,100]{0,1:T(8,128)S(1)} %copy-done, f32[1024]{0:T(1024)S(1)} %copy-done.1), kind=kOutput, calls=%fused_computation.47 | convolution fusion | flops 3357491200 | bytes 40931328 | tf_op jit(solution)/shard_map/dot_general | solution.py:19
  165.1 17.7 %convolution_bitcast_fusion.5 = f32[16384,100]{0,1:T(8,128)} fusion(bf16[16384,1024]{1,0:T(8,128)(2,1)} %param.4, f32[1024,100]{0,1:T(8,128)S(1)} %fusion.81), kind=kOutput, calls=%fused_computation.5 | convolution fusion | flops 3355545600 | bytes 40517632 | tf_op jit(solution)/shard_map/dot_general | solution.py:22
  182.9 0.1 all-reduce.10.cloned.1.call-update
  182.9 0.1 all-reduce.12.cloned.1.call-start
  183.0 105.9 %all-reduce.10.cloned.1.call-done = f32[16384,100]{0,1:T(8,128)} async-done(((f32[16384,100]{0,1:T(8,128)}), f32[16384,100]{0,1:T(8,128)}) %all-reduce.10.cloned.1.call-update) | async-done | bytes 6553616 | tf_op jit(solution)/shard_map/psum | solution.py:23
  288.9 17.2 %multiply_add_fusion.4 = (f32[1024,100]{0,1:T(8,128)S(1)}, bf16[1024,100]{0,1:T(8,128)(2,1)S(1)}) fusion(f32[1024,100]{0,1:T(8,128)S(1)} %copy-done, f32[1024,100]{0,1:T(8,128)S(1)} %fusion.81, bf16[16384,1024]{1,0:T(8,128)(2,1)} %param.4, f32[16384,100]{0,1:T(8,128)} %sub.39, f32[16384,100]{0,1:T(8,128)} %all-reduce.10.cloned.1.call-done, ...), kind=kOutput, calls=%fused_computation.52 | convolution fusion | flops 3361280000 | bytes 48099328 | tf_op jit(solution)/shard_map/dot_general | solution.py:19
  306.1 17.6 %convolution_bitcast_fusion.4 = f32[16384,100]{0,1:T(8,128)} fusion(bf16[16384,1024]{1,0:T(8,128)(2,1)} %param.4, bf16[1024,100]{0,1:T(8,128)(2,1)S(1)} %get-tuple-element.3), kind=kOutput, calls=%fused_computation.4 | convolution fusion | flops 3355443200 | bytes 40312832 | tf_op jit(solution)/shard_map/dot_general | solution.py:22
  323.8 0.1 all-reduce.12.cloned.1.call-update
  323.8 0.6 all-reduce.14.cloned.1.call-start
  324.4 105.3 %all-reduce.12.cloned.1.call-done = f32[16384,100]{0,1:T(8,128)} async-done(((f32[16384,100]{0,1:T(8,128)}), f32[16384,100]{0,1:T(8,128)}) %all-reduce.12.cloned.1.call-update) | async-done | bytes 6553616 | tf_op jit(solution)/shard_map/psum | solution.py:23
  429.7 10.9 %multiply_subtract_fusion.4 = f32[16384,100]{0,1:T(8,128)} fusion(f32[16384,100]{0,1:T(8,128)} %all-reduce.12.cloned.1.call-done, f32[16384,100]{0,1:T(8,128)} %sub.39, f32[16384,100]{0,1:T(8,128)} %all-reduce.10.cloned.1.call-done), kind=kLoop, calls=%fused_computation.10 | loop fusion | flops 6553600 | bytes 26214400 | tf_op jit(solution)/shard_map/sub | solution.py:23
  440.6 15.1 %fusion.69 = f32[1024,100]{0,1:T(8,128)S(1)} fusion(bf16[16384,1024]{1,0:T(8,128)(2,1)} %param.4, f32[16384,100]{0,1:T(8,128)} %multiply_subtract_fusion.4, f32[1024,100]{0,1:T(8,128)S(1)} %get-tuple-element.2, f32[1024]{0:T(1024)S(1)} %copy-done.1), kind=kOutput, calls=%fused_computation.43 | convolution fusion | flops 3357491200 | bytes 40931328 | tf_op jit(solution)/shard_map/dot_general | solution.py:19
  455.7 17.7 %convolution_bitcast_fusion.3 = f32[16384,100]{0,1:T(8,128)} fusion(bf16[16384,1024]{1,0:T(8,128)(2,1)} %param.4, f32[1024,100]{0,1:T(8,128)S(1)} %fusion.69), kind=kOutput, calls=%fused_computation.3 | convolution fusion | flops 3355545600 | bytes 40517632 | tf_op jit(solution)/shard_map/dot_general | solution.py:22
  473.5 0.1 all-reduce.14.cloned.1.call-update
  473.5 0.1 all-reduce.16.cloned.1.call-start
  473.6 105.9 %all-reduce.14.cloned.1.call-done = f32[16384,100]{0,1:T(8,128)} async-done(((f32[16384,100]{0,1:T(8,128)}), f32[16384,100]{0,1:T(8,128)}) %all-reduce.14.cloned.1.call-update) | async-done | bytes 6553616 | tf_op jit(solution)/shard_map/psum | solution.py:23
  579.5 17.2 %multiply_add_fusion.2 = (f32[1024,100]{0,1:T(8,128)S(1)}, bf16[1024,100]{0,1:T(8,128)(2,1)S(1)}) fusion(f32[1024,100]{0,1:T(8,128)S(1)} %get-tuple-element.2, f32[1024,100]{0,1:T(8,128)S(1)} %fusion.69, bf16[16384,1024]{1,0:T(8,128)(2,1)} %param.4, f32[16384,100]{0,1:T(8,128)} %multiply_subtract_fusion.4, f32[16384,100]{0,1:T(8,128)} %all-reduce.14.cloned.1.call-done, ...), kind=kOutput, calls=%fused_computation.50 | convolution fusion | flops 3361280000 | bytes 48099328 | tf_op jit(solution)/shard_map/dot_general | solution.py:19
  596.7 17.6 %convolution_bitcast_fusion.2 = f32[16384,100]{0,1:T(8,128)} fusion(bf16[16384,1024]{1,0:T(8,128)(2,1)} %param.4, bf16[1024,100]{0,1:T(8,128)(2,1)S(1)} %get-tuple-element.5), kind=kOutput, calls=%fused_computation.2 | convolution fusion | flops 3355443200 | bytes 40312832 | tf_op jit(solution)/shard_map/dot_general | solution.py:22
  614.3 0.1 all-reduce.16.cloned.1.call-update
  614.4 0.2 all-reduce.18.cloned.1.call-start
  614.6 105.7 %all-reduce.16.cloned.1.call-done = f32[16384,100]{0,1:T(8,128)} async-done(((f32[16384,100]{0,1:T(8,128)}), f32[16384,100]{0,1:T(8,128)}) %all-reduce.16.cloned.1.call-update) | async-done | bytes 6553616 | tf_op jit(solution)/shard_map/psum | solution.py:23
  720.3 10.9 %multiply_subtract_fusion.2 = f32[16384,100]{0,1:T(8,128)} fusion(f32[16384,100]{0,1:T(8,128)} %all-reduce.16.cloned.1.call-done, f32[16384,100]{0,1:T(8,128)} %multiply_subtract_fusion.4, f32[16384,100]{0,1:T(8,128)} %all-reduce.14.cloned.1.call-done), kind=kLoop, calls=%fused_computation.8 | loop fusion | flops 6553600 | bytes 26214400 | tf_op jit(solution)/shard_map/sub | solution.py:23
  731.2 15.1 %fusion.57 = f32[1024,100]{0,1:T(8,128)S(1)} fusion(bf16[16384,1024]{1,0:T(8,128)(2,1)} %param.4, f32[16384,100]{0,1:T(8,128)} %multiply_subtract_fusion.2, f32[1024,100]{0,1:T(8,128)S(1)} %get-tuple-element.4, f32[1024]{0:T(1024)S(1)} %copy-done.1), kind=kOutput, calls=%fused_computation.39 | convolution fusion | flops 3357491200 | bytes 40931328 | tf_op jit(solution)/shard_map/dot_general | solution.py:19
  746.3 17.7 %convolution_bitcast_fusion.1 = f32[16384,100]{0,1:T(8,128)} fusion(bf16[16384,1024]{1,0:T(8,128)(2,1)} %param.4, f32[1024,100]{0,1:T(8,128)S(1)} %fusion.57), kind=kOutput, calls=%fused_computation.1 | convolution fusion | flops 3355545600 | bytes 40517632 | tf_op jit(solution)/shard_map/dot_general | solution.py:22
  764.0 0.1 all-reduce.18.cloned.1.call-update
  764.1 0.3 all-reduce.20.cloned.1.call-start
  764.4 105.7 %all-reduce.18.cloned.1.call-done = f32[16384,100]{0,1:T(8,128)} async-done(((f32[16384,100]{0,1:T(8,128)}), f32[16384,100]{0,1:T(8,128)}) %all-reduce.18.cloned.1.call-update) | async-done | bytes 6553616 | tf_op jit(solution)/shard_map/psum | solution.py:23
  870.1 20.5 %multiply_add_fusion = (f32[1024,100]{0,1:T(8,128)}, bf16[1024,100]{0,1:T(8,128)(2,1)S(1)}) fusion(f32[1024,100]{0,1:T(8,128)S(1)} %get-tuple-element.4, f32[1024,100]{0,1:T(8,128)S(1)} %fusion.57, bf16[16384,1024]{1,0:T(8,128)(2,1)} %param.4, f32[16384,100]{0,1:T(8,128)} %multiply_subtract_fusion.2, f32[16384,100]{0,1:T(8,128)} %all-reduce.18.cloned.1.call-done, ...), kind=kOutput, calls=%fused_computation.48 | convolution fusion | flops 3361280000 | bytes 48099328 | tf_op jit(solution)/shard_map/dot_general | solution.py:19
  890.6 17.6 %convolution_bitcast_fusion = f32[16384,100]{0,1:T(8,128)} fusion(bf16[16384,1024]{1,0:T(8,128)(2,1)} %param.4, bf16[1024,100]{0,1:T(8,128)(2,1)S(1)} %get-tuple-element.7), kind=kOutput, calls=%fused_computation | convolution fusion | flops 3355443200 | bytes 40312832 | tf_op jit(solution)/shard_map/dot_general | solution.py:22
  908.2 0.1 all-reduce.20.cloned.1.call-update
  908.3 105.9 %all-reduce.20.cloned.1.call-done = f32[16384,100]{0,1:T(8,128)} async-done(((f32[16384,100]{0,1:T(8,128)}), f32[16384,100]{0,1:T(8,128)}) %all-reduce.20.cloned.1.call-update) | async-done | bytes 6553616 | tf_op jit(solution)/shard_map/psum | solution.py:23
  1014.2 10.9 %multiply_subtract_fusion = f32[16384,100]{0,1:T(8,128)} fusion(f32[16384,100]{0,1:T(8,128)} %all-reduce.20.cloned.1.call-done, f32[16384,100]{0,1:T(8,128)} %multiply_subtract_fusion.2, f32[16384,100]{0,1:T(8,128)} %all-reduce.18.cloned.1.call-done), kind=kLoop, calls=%fused_computation.6 | loop fusion | flops 6553600 | bytes 26214400 | tf_op jit(solution)/shard_map/sub | solution.py:23
Async XLA Ops:
  7.2 134.4 %all-reduce.8.cloned.1.call-start = ((), (), s32[]{:S(2)}) async-start(), calls=%async_computation | async-start | bytes 13631488 | tf_op jit(solution)/shard_map/psum | solution.py:17
  31.3 118.8 %copy-start = (f32[1024,100]{0,1:T(8,128)S(1)}, f32[1024,100]{0,1:T(8,128)}, u32[]{:S(2)}) copy-start(f32[1024,100]{0,1:T(8,128)} %param.6) | copy-start | bytes 1228804
  31.3 118.8 %copy-start.1 = (f32[1024]{0:T(1024)S(1)}, f32[1024]{0:T(1024)}, u32[]{:S(2)}) copy-start(f32[1024]{0:T(1024)} %param.7) | copy-start | bytes 12292
  31.3 257.6 %all-reduce.10.cloned.1.call-start = ((), (), s32[]{:S(2)}) async-start(), calls=%async_computation.1 | async-start | bytes 13631488 | tf_op jit(solution)/shard_map/psum | solution.py:23
  182.9 246.8 %all-reduce.12.cloned.1.call-start = ((), (), s32[]{:S(2)}) async-start(), calls=%async_computation.2 | async-start | bytes 13631488 | tf_op jit(solution)/shard_map/psum | solution.py:23
  323.8 255.6 %all-reduce.14.cloned.1.call-start = ((), (), s32[]{:S(2)}) async-start(), calls=%async_computation.3 | async-start | bytes 13631488 | tf_op jit(solution)/shard_map/psum | solution.py:23
  473.5 246.8 %all-reduce.16.cloned.1.call-start = ((), (), s32[]{:S(2)}) async-start(), calls=%async_computation.4 | async-start | bytes 13631488 | tf_op jit(solution)/shard_map/psum | solution.py:23
  614.4 255.7 %all-reduce.18.cloned.1.call-start = ((), (), s32[]{:S(2)}) async-start(), calls=%async_computation.5 | async-start | bytes 13631488 | tf_op jit(solution)/shard_map/psum | solution.py:23
  764.1 250.1 %all-reduce.20.cloned.1.call-start = ((), (), s32[]{:S(2)}) async-start(), calls=%async_computation.6 | async-start | bytes 13631488 | tf_op jit(solution)/shard_map/psum | solution.py:23
Sparse Core Ops, SparseCore 0:
  31.4 110.1 all-reduce.7
  183.1 105.7 all-reduce.9
  323.9 105.7 all-reduce.11
  473.7 105.7 all-reduce.13
  614.5 105.7 all-reduce.15
  764.2 105.8 all-reduce.17
  908.4 105.7 all-reduce.19
where the time goes:
time: 1040 us; the launch traced here: 1030 us
  waiting for transfers between devices  745 us (72%)
  matrix products  230 us (22%)
  other arithmetic  41.1 us (4%)
  between operations  14.4 us (1%)
    psum x6, waiting for transfers between devices, local_solve(): residual = residual - MIX_WEIGHT * lax.psum(contrib, 'feat')  634 us
    psum x1, waiting for transfers between devices, local_solve(): residual = targets - lax.psum(partial, 'feat')  110 us
    dot_general x6, matrix products, local_solve(): jnp.dot(design, update.astype(jnp.bfloat16), preferred_element_type=jnp.f...  106 us
    dot_general x6, matrix products, local_solve(): lax.dot_general(design, residual.astype(jnp.bfloat16), (((0,), (0,)), (()...  100 us
    sub x3, other arithmetic, local_solve(): residual = residual - MIX_WEIGHT * lax.psum(contrib, 'feat')  32.6 us
    dot_general x1, matrix products, local_solve(): jnp.dot(design, weights.astype(jnp.bfloat16), preferred_element_type=jnp....  24 us
  transfers between devices with their start and end apart: 7, of which 7 were waited for; matrix products, arithmetic and copies ran while one was open for 0% of the time, Pallas kernels for 0%

commit v1 on v0

v1 whole, which is shorter than its diff:
```python
import functools
import math

import jax
import jax.numpy as jnp
from jax import lax
from jax.experimental import pallas as pl
from jax.experimental.pallas import tpu as pltpu
from jax.sharding import PartitionSpec as P

SWEEPS = 6
RIDGE_COEF = 1.0
MIX_WEIGHT = 0.75
CHUNKS = 4
CORES = 2
MESH = pl.DeviceIdType.MESH


class _Copy:
    def __init__(self, *args):
        self.args = args

    def _make(self):
        src, dst, send_sem, recv_sem, device = self.args
        return pltpu.make_async_remote_copy(src_ref=src, dst_ref=dst, send_sem=send_sem, recv_sem=recv_sem,
                                            device_id=device, device_id_type=MESH)

    def start(self):
        self._make().start()

    def wait_recv(self):
        self._make().wait_recv()

    def wait_send(self):
        self._make().wait_send()


def _up(v, m):
    return (v + m - 1) // m * m


def _split(v, m):
    top = _up(v // 2, m)
    return top, v - top


def _kernel(n, side, kf, kb, x_hbm, y_ref, w0_ref, eta_ref, w_ref, r_hbm,
            xv, c_buf, d_buf, far1, near1, far2, near2, t_buf, rt, own, gacc, dwt,
            send, recv, load_sem, out_sem, free):
    q_all = CHUNKS
    rows = n // q_all
    half = rows // CORES
    w1 = half // side
    w2 = w1 // side
    ka, kc = _split(kf, 8)
    ba, bc = _split(kb, 16)
    last = SWEEPS

    me = lax.axis_index('feat')
    core = lax.rem(me, CORES)
    px = lax.rem(me // CORES, side)
    py = me // (CORES * side)
    peer = 1 - core
    hbase = pl.multiple_of(core * half, half)
    pbase = pl.multiple_of(peer * half, half)

    def dev(yy, xx, cc):
        return {'feat': (yy * side + xx) * CORES + cc}

    def step(v, s):
        return lax.rem(v + (s + side), side)

    xp, xm = dev(py, step(px, 1), core), dev(py, step(px, -1), core)
    yp, ym = dev(step(py, 1), px, core), dev(step(py, -1), px, core)
    mate = dev(py, px, peer)
    rings = [((px, xp, xm), (py, yp, ym)) if q % 2 == 0 else ((py, yp, ym), (px, xp, xm)) for q in range(q_all)]

    barrier = pltpu.get_barrier_semaphore()
    for d in (xp, xm, yp, ym, mate):
        pl.semaphore_signal(barrier, inc=1, device_id=d, device_id_type=MESH)

    def load(q, cc):
        def one(i, carry):
            a, b = i // side, lax.rem(i, side)
            d = ((b * side + a) if q % 2 == 0 else (a * side + b)) * CORES + cc
            src = x_hbm.at[pl.ds(pl.multiple_of(d * (q_all * w2) + q * w2, w2), w2), :]
            dst = xv.at[q, pl.ds(pl.multiple_of(cc * half + i * w2, w2), w2), :]
            pltpu.make_async_copy(src, dst, load_sem.at[q, cc]).start()
            return carry
        lax.fori_loop(0, side * side, one, 0)

    def load_wait(q, cc, base):
        ref = xv.at[q, pl.ds(base, half), :]
        pltpu.make_async_copy(ref, ref, load_sem.at[q, cc]).wait()

    for q in range(q_all):
        load(q, peer)
        load(q, core)

    own[...] = y_ref[...]
    w_ref[...] = w0_ref[...]
    dwt[...] = w0_ref[...].astype(jnp.bfloat16)
    pl.semaphore_wait(barrier, 5)

    def rc(src, dst, q, k, device):
        return _Copy(src, dst, send.at[q, k], recv.at[q, k], device)

    def lanes(base, width):
        return pl.ds(pl.multiple_of(base, 128), width)

    def c_d2d(q):
        return rc(c_buf.at[q, :, lanes(pbase, half)], d_buf.at[q], q, 0, mate)

    def rs_copies(q, stage):
        idx, plus, minus = rings[q][stage]
        if stage == 0:
            src, width, far, near = d_buf.at[q], w1, far1, near1
        else:
            src, width, far, near = t_buf.at[q], w2, far2, near2
        k0 = 1 + 6 * stage

        def cut(i, lo, size):
            return src.at[pl.ds(lo, size), lanes(i * width, width)]

        f, p, m = step(idx, 2), step(idx, 1), step(idx, -1)
        return dict(
            far=(rc(cut(f, 0, ka), far.at[q, 0], q, k0, plus),
                 rc(cut(f, ka, kc), far.at[q, 1, pl.ds(0, kc), :], q, k0 + 1, minus)),
            plain=(rc(cut(p, ka, kc), near.at[q, 0, pl.ds(ka, kc), :], q, k0 + 2, plus),
                   rc(cut(m, 0, ka), near.at[q, 1, pl.ds(0, ka), :], q, k0 + 3, minus)),
            aug=(rc(cut(p, 0, ka), near.at[q, 0, pl.ds(0, ka), :], q, k0 + 4, plus),
                 rc(cut(m, ka, kc), near.at[q, 1, pl.ds(ka, kc), :], q, k0 + 5, minus)))

    def start(copies):
        for c in copies:
            c.start()

    def recv_wait(copies):
        for c in copies:
            c.wait_recv()

    def send_wait(copies):
        for c in copies:
            c.wait_send()

    def rs_first(q, stage):
        cp = rs_copies(q, stage)
        start(cp['far'])
        start(cp['plain'])

    def rs_mid(q, stage):
        idx = rings[q][stage][0]
        src, width, far = (d_buf, w1, far1) if stage == 0 else (t_buf, w2, far2)
        cp = rs_copies(q, stage)
        p, m = step(idx, 1), step(idx, -1)
        cp['far'][0].wait_recv()
        at = (q, pl.ds(0, ka), lanes(p * width, width))
        src[at] = src[at] + far[q, 0]
        cp['aug'][0].start()
        cp['far'][1].wait_recv()
        at = (q, pl.ds(ka, kc), lanes(m * width, width))
        src[at] = src[at] + far[q, 1, pl.ds(0, kc), :]
        cp['aug'][1].start()

    def rs_total(q, stage):
        idx = rings[q][stage][0]
        src, width, near = (d_buf, w1, near1) if stage == 0 else (t_buf, w2, near2)
        cp = rs_copies(q, stage)
        recv_wait(cp['plain'])
        recv_wait(cp['aug'])
        return src[q, :, lanes(idx * width, width)] + (near[q, 0] + near[q, 1])

    def ag_copies(q, wide):
        (i1, p1, m1), (i2, p2, m2) = rings[q]
        buf, top, low = (c_buf, ka, kc) if wide else (rt, ba, bc)
        b0 = hbase + i1 * w1

        def cut(base, width, part):
            r = {None: slice(None), 0: pl.ds(0, top), 1: pl.ds(top, low)}[part]
            return buf.at[q, r, lanes(base, width)]

        def to(base, width, part, k, device):
            ref = cut(base, width, part)
            return rc(ref, ref, q, k, device)

        a, b = step(i2, -1), step(i2, 1)
        c, d, e = step(i1, -1), step(i1, 1), step(i1, 2)
        out = dict(
            n1=(to(b0 + i2 * w2, w2, None, 13, p2), to(b0 + i2 * w2, w2, None, 14, m2)),
            f1=(to(b0 + a * w2, w2, 0, 15, p2), to(b0 + b * w2, w2, 1, 16, m2)),
            n2=(to(b0, w1, None, 17, p1), to(b0, w1, None, 18, m1)),
            f2=(to(hbase + c * w1, w1, 0, 19, p1), to(hbase + d * w1, w1, 1, 20, m1)))
        out['x'] = tuple(to(hbase + i * w1, w1, None, 21 + j, mate) for j, i in enumerate((i1, c, d, e)))
        return out

    def ag_first(q, wide):
        start(ag_copies(q, wide)['n1'])

    def ag_fwd1(q, wide):
        cp = ag_copies(q, wide)
        for a, b in zip(cp['n1'], cp['f1']):
            a.wait_recv()
            b.start()

    def ag_second(q, wide):
        cp = ag_copies(q, wide)
        recv_wait(cp['f1'])
        start(cp['n2'])
        if wide:
            pl.semaphore_wait(free.at[q], 1)
        cp['x'][0].start()

    def ag_fwd2(q, wide):
        cp = ag_copies(q, wide)
        for a, b in zip(cp['n2'], cp['f2']):
            a.wait_recv()
            b.start()
        start(cp['x'][1:3])

    def ag_last(q, wide):
        cp = ag_copies(q, wide)
        recv_wait(cp['f2'])
        cp['x'][3].start()

    def ag_mate(q, wide):
        recv_wait(ag_copies(q, wide)['x'])

    def partial_product(q, base):
        v = lax.dot_general(dwt[...], xv[q, pl.ds(base, half), :], (((1,), (1,)), ((), ())),
                            preferred_element_type=jnp.float32)
        c_buf[q, :, pl.ds(base, half)] = v[:kf]

    def gradient(q, base):
        gacc[...] += jnp.dot(rt[q, :, pl.ds(base, half)], xv[q, pl.ds(base, half), :],
                             preferred_element_type=jnp.float32)

    def sweep(t, carry):
        first = t == 0
        scale = jnp.where(first, jnp.float32(1.0), jnp.float32(MIX_WEIGHT))

        def gathers(f, q):
            @pl.when(t < last)
            def _():
                f(q, False)

            @pl.when(t == last)
            def _():
                f(q, True)

        def product(q, mates):
            @pl.when(first)
            def _():
                load_wait(q, peer if mates else core, pbase if mates else hbase)
            partial_product(q, pbase if mates else hbase)
            if mates:
                c_d2d(q).start()

        def pair_sum(q):
            c_d2d(q).wait_recv()
            d_buf[q] = d_buf[q] + c_buf[q, :, pl.ds(hbase, half)]
            rs_first(q, 0)

        def sent(q, stage):
            cp = rs_copies(q, stage)
            for key in ('far', 'plain', 'aug'):
                send_wait(cp[key])

        def ring_sum(q):
            t_buf[q] = rs_total(q, 0)
            rs_first(q, 1)
            c_d2d(q).wait_send()

            @pl.when(t == last)
            def _():
                pl.semaphore_signal(free.at[q], inc=1, device_id=mate, device_id_type=MESH)

        def finish(q):
            fresh = own[q, pl.ds(0, kf), :] - scale * rs_total(q, 1)
            own[q, pl.ds(0, kf), :] = fresh
            sent(q, 0)
            idx = rings[q]
            at = lanes(hbase + idx[0][0] * w1 + idx[1][0] * w2, w2)

            @pl.when(t < last)
            def _():
                rt[q, :, at] = own[q].astype(jnp.bfloat16)

            @pl.when(t == last)
            def _():
                c_buf[q, :, at] = own[q, pl.ds(0, kf), :]
            gathers(ag_first, q)

        product(0, True)
        product(0, False)
        product(1, True)
        pair_sum(0)
        product(1, False)
        pair_sum(1)
        product(2, True)
        product(2, False)
        rs_mid(0, 0)
        product(3, True)
        rs_mid(1, 0)
        product(3, False)
        pair_sum(2)
        pair_sum(3)
        ring_sum(0)
        ring_sum(1)
        rs_mid(0, 1)
        rs_mid(1, 1)
        rs_mid(2, 0)
        rs_mid(3, 0)
        finish(0)
        finish(1)
        gathers(ag_fwd1, 0)
        gathers(ag_fwd1, 1)
        ring_sum(2)
        ring_sum(3)
        gathers(ag_second, 0)
        gathers(ag_second, 1)
        rs_mid(2, 1)
        rs_mid(3, 1)
        gathers(ag_fwd2, 0)
        gathers(ag_fwd2, 1)
        finish(2)
        finish(3)
        gathers(ag_fwd1, 2)
        gathers(ag_fwd1, 3)
        gathers(ag_last, 0)
        gathers(ag_last, 1)
        gathers(ag_second, 2)
        gathers(ag_second, 3)

        @pl.when(t < last)
        def _():
            gacc[...] = jnp.zeros_like(gacc)
            gradient(0, hbase)
            gradient(1, hbase)
        gathers(ag_mate, 0)
        gathers(ag_mate, 1)
        gathers(ag_fwd2, 2)
        gathers(ag_fwd2, 3)

        @pl.when(t < last)
        def _():
            gradient(0, pbase)
            gradient(1, pbase)
        gathers(ag_last, 2)
        gathers(ag_last, 3)

        @pl.when(t < last)
        def _():
            gradient(2, hbase)
            gradient(3, hbase)
        gathers(ag_mate, 2)
        gathers(ag_mate, 3)

        def drain(q, wide):
            cp = ag_copies(q, wide)
            for key in ('n1', 'f1', 'n2', 'f2', 'x'):
                send_wait(cp[key])

        for q in range(q_all):
            sent(q, 1)
            gathers(drain, q)

        @pl.when(t < last)
        def _():
            gradient(2, pbase)
            gradient(3, pbase)
            update = eta_ref[...] * (gacc[...] * (1.0 / n) - (RIDGE_COEF / n) * w_ref[...])
            w_ref[...] = w_ref[...] + MIX_WEIGHT * update
            dwt[...] = update.astype(jnp.bfloat16)
        return carry

    lax.fori_loop(0, last + 1, sweep, 0)

    def piece(i, carry):
        for q in range(q_all):
            cc, j = i // (side * side), lax.rem(i, side * side)
            a, b = j // side, lax.rem(j, side)
            d = ((b * side + a) if q % 2 == 0 else (a * side + b)) * CORES + cc
            pltpu.make_async_copy(c_buf.at[q, :, lanes(i * w2, w2)],
                                  r_hbm.at[:, lanes((d * q_all + q) * w2, w2)], out_sem).start()
        return carry
    lax.fori_loop(0, CORES * side * side, piece, 0)
    for q in range(q_all):
        pltpu.make_async_copy(c_buf.at[q], c_buf.at[q], out_sem).wait()


def solution(mesh):
    group = mesh.shape['feat']
    side = math.isqrt(group // CORES)

    def local_solve(design, targets, weights, step_sizes):
        n, feats = design.shape
        k = targets.shape[1]
        kf, kb = _up(k, 8), _up(k, 16)
        rows = n // CHUNKS
        half = rows // CORES
        w1 = half // side
        w2 = w1 // side
        ka = _split(kf, 8)[0]
        share = n // group
        me = lax.axis_index('feat')
        mine = lax.dynamic_slice_in_dim(targets, me * share, share, 0)
        mine = jnp.pad(jnp.swapaxes(mine.reshape(CHUNKS, w2, k), 1, 2), ((0, 0), (0, kb - k), (0, 0)))
        wt = jnp.pad(weights.T, ((0, kb - k), (0, 0)))
        f32, bf16 = jnp.float32, jnp.bfloat16
        vm = pl.BlockSpec(memory_space=pltpu.VMEM)
        hb = pl.BlockSpec(memory_space=pl.ANY)
        w_out, r_out = pl.pallas_call(
            functools.partial(_kernel, n, side, kf, kb),
            out_shape=(jax.ShapeDtypeStruct((kb, feats), f32), jax.ShapeDtypeStruct((kf, n), f32)),
            in_specs=[hb, vm, vm, vm],
            out_specs=(vm, hb),
            scratch_shapes=[
                pltpu.VMEM((CHUNKS, rows, feats), bf16),
                pltpu.VMEM((CHUNKS, kf, rows), f32),
                pltpu.VMEM((CHUNKS, kf, half), f32),
                pltpu.VMEM((CHUNKS, 2, ka, w1), f32),
                pltpu.VMEM((CHUNKS, 2, kf, w1), f32),
                pltpu.VMEM((CHUNKS, 2, ka, w2), f32),
                pltpu.VMEM((CHUNKS, 2, kf, w2), f32),
                pltpu.VMEM((CHUNKS, kf, w1), f32),
                pltpu.VMEM((CHUNKS, kb, rows), bf16),
                pltpu.VMEM((CHUNKS, kb, w2), f32),
                pltpu.VMEM((kb, feats), f32),
                pltpu.VMEM((kb, feats), bf16),
                pltpu.SemaphoreType.DMA((CHUNKS, 25)),
                pltpu.SemaphoreType.DMA((CHUNKS, 25)),
                pltpu.SemaphoreType.DMA((CHUNKS, CORES)),
                pltpu.SemaphoreType.DMA,
                pltpu.SemaphoreType.REGULAR((CHUNKS,)),
            ],
            compiler_params=pltpu.CompilerParams(
                collective_id=0, has_side_effects=True, vmem_limit_bytes=67043328),
        )(design, mine, wt, step_sizes[None, :])
        return w_out[:k].T, r_out[:k].T

    return jax.shard_map(
        local_solve,
        mesh=mesh,
        in_specs=(P('prob', 'feat'), P('prob', None), P(('prob', 'feat'), None), P(('prob', 'feat'))),
        out_specs=(P(('prob', 'feat'), None), P('prob', None)),
        check_vma=False,
    )
```

time: 1040 us -> 424 us (0.41)
  waiting for transfers between devices: 745 us -> 0 us
  Pallas kernels: 0 us -> 411 us
  matrix products: 230 us -> 0 us
  other arithmetic: 41.1 us -> 0 us
  between operations: 14.4 us -> 0.66 us
  local copies, waits for them, and re-layouts: 0.01 us -> 11.7 us
    psum x7 -> x0, waiting for transfers between devices: 744 us -> none  [the longest x6 634 us: local_solve(): residual = residual - MIX_WEIGHT * lax.psum(contrib, 'feat')]
    pallas_call x0 -> x1, Pallas kernels: none -> 411 us  [local_solve(): pl.pallas_call(functools.partial(_kernel, n, side, kf, kb), out_shape=(ja...]
    dot_general x13 -> x0, matrix products: 230 us -> none  [the longest x6 106 us: local_solve(): jnp.dot(design, update.astype(jnp.bfloat16), preferred_element_type=jnp.f...]
    sub x4 -> x0, other arithmetic: 41.1 us -> none  [the longest x3 32.6 us: local_solve(): residual = residual - MIX_WEIGHT * lax.psum(contrib, 'feat')]
  transfers between devices with their start and end apart: 7 -> 0, of which waited for: 7 -> 0; matrix products, arithmetic and copies ran while one was open for 0% -> 0% of each run, Pallas kernels for 0% -> 0%
where the time goes in v1:
time: 424 us; the launch traced here: 423 us
  Pallas kernels  411 us (97%)
  local copies, waits for them, and re-layouts  11.7 us (3%)
    pallas_call x1, Pallas kernels, local_solve(): pl.pallas_call(functools.partial(_kernel, n, side, kf, kb), out_shape=(ja...  411 us

profile of v1, /device:TPU:97, one launch (start us, length us, event | category | flops | bytes accessed | tf_op | source)
XLA Modules:
  0.0 423.3 jit_solution(28711336330226276)
XLA Ops:
  0.6 1.0 constant_dynamic-slice_fusion
  1.6 0.1 reshape.7
  1.7 0.7 pad.8.y_ref
  2.4 1.8 pad.9.w0_ref
  4.2 411.0 %shard_map.59 = (f32[112,1024]{1,0:T(8,128)}, f32[104,16384]{1,0:T(8,128)}) custom-call(bf16[16384,1024]{1,0:T(8,128)(2,1)} %x_hbm.1, f32[4,112,128]{2,1,0:T(8,128)} %pad.8.y_ref, f32[112,1024]{1,0:T(8,128)} %pad.9.w0_ref, f32[1,1024]{1,0:T(1,128)} %bitcast.13), custom_call_target="tpu_custom_call" | custom-call | tf_op jit(solution)/shard_map/pallas_call | solution.py:412
  415.2 1.8 slice_bitcast_fusion.1
  417.0 6.3 %slice_bitcast_fusion = f32[16384,100]{0,1:T(8,128)} fusion(f32[104,16384]{1,0:T(8,128)} %get-tuple-element.5), kind=kLoop, calls=%fused_computation | loop fusion | bytes 13107200 | tf_op jit(solution)/shard_map/transpose | solution.py:439
  (1 shorter events, 0.0 us)

commit v2 on v1

--- a/solution.py
+++ b/solution.py
@@ -13,6 +13,12 @@
 MIX_WEIGHT = 0.75
 CHUNKS = 4
 CORES = 2
+SCHEDULE = (
+    'A0 B0 A1 B1', 'S0 S1 P0 O0', 'P1 N0 O1 N1', 'A2 B2 A3 B3', 'a0 a1 P2 O2', 'S2 S3 P3 O3', 'p0 o0 p1 o1',
+    'N2 N3 s0 s1', 'T0 T1 p2 o2', 'p3 o3 s2 s3', 'a2 a3 b0 b1', 'T2 T3 F0 F1', 'b2 b3 c0 c1', 'F2 F3 d0 d1',
+    'c2 c3 e0 e1', 'k0 k1 G0 G1', 'd2 d3 m0 m1', 'f0 f1 H0 H1', 'e2 e3 k2 k3', 'g0 g1 n0 n1', 'h0 h1 G2 G3',
+    'f2 f3 m2 m3', 'H2 H3 g2 g3', 'D0 D1 D2 D3', 'n2 n3 h2 h3',
+)
 MESH = pl.DeviceIdType.MESH
 
 
@@ -98,6 +104,7 @@
         load(q, core)
 
     own[...] = y_ref[...]
+    gacc[...] = jnp.zeros_like(gacc)
     w_ref[...] = w0_ref[...]
     dwt[...] = w0_ref[...].astype(jnp.bfloat16)
     pl.semaphore_wait(barrier, 5)
@@ -108,8 +115,13 @@
     def lanes(base, width):
         return pl.ds(pl.multiple_of(base, 128), width)
 
-    def c_d2d(q):
-        return rc(c_buf.at[q, :, lanes(pbase, half)], d_buf.at[q], q, 0, mate)
+    def blocks(q):
+        idx = rings[q][0][0]
+        return step(idx, 2), step(idx, 1), step(idx, -1), idx
+
+    def c_d2d(q, j):
+        at = blocks(q)[j] * w1
+        return rc(c_buf.at[q, :, lanes(pbase + at, w1)], d_buf.at[q, :, lanes(at, w1)], q, j, mate)
 
     def rs_copies(q, stage):
         idx, plus, minus = rings[q][stage]
@@ -117,7 +129,7 @@
             src, width, far, near = d_buf.at[q], w1, far1, near1
         else:
             src, width, far, near = t_buf.at[q], w2, far2, near2
-        k0 = 1 + 6 * stage
+        k0 = 4 + 6 * stage
 
         def cut(i, lo, size):
             return src.at[pl.ds(lo, size), lanes(i * width, width)]
@@ -142,11 +154,6 @@
     def send_wait(copies):
         for c in copies:
             c.wait_send()
-
-    def rs_first(q, stage):
-        cp = rs_copies(q, stage)
-        start(cp['far'])
-        start(cp['plain'])
 
     def rs_mid(q, stage):
         idx = rings[q][stage][0]
@@ -185,54 +192,75 @@
 
         a, b = step(i2, -1), step(i2, 1)
         c, d, e = step(i1, -1), step(i1, 1), step(i1, 2)
-        out = dict(
-            n1=(to(b0 + i2 * w2, w2, None, 13, p2), to(b0 + i2 * w2, w2, None, 14, m2)),
-            f1=(to(b0 + a * w2, w2, 0, 15, p2), to(b0 + b * w2, w2, 1, 16, m2)),
-            n2=(to(b0, w1, None, 17, p1), to(b0, w1, None, 18, m1)),
-            f2=(to(hbase + c * w1, w1, 0, 19, p1), to(hbase + d * w1, w1, 1, 20, m1)))
-        out['x'] = tuple(to(hbase + i * w1, w1, None, 21 + j, mate) for j, i in enumerate((i1, c, d, e)))
-        return out
+        pieces = (i2, a, b, step(i2, 2))
+        return dict(
+            n1=(to(b0 + i2 * w2, w2, None, 16, p2), to(b0 + i2 * w2, w2, None, 17, m2)),
+            f1=(to(b0 + a * w2, w2, 0, 18, p2), to(b0 + b * w2, w2, 1, 19, m2)),
+            n2=[(to(b0 + i * w2, w2, None, 20 + 2 * j, p1), to(b0 + i * w2, w2, None, 21 + 2 * j, m1))
+                for j, i in enumerate(pieces)],
+            f2=[(to(hbase + c * w1 + i * w2, w2, 0, 28 + 2 * j, p1), to(hbase + d * w1 + i * w2, w2, 1, 29 + 2 * j, m1))
+                for j, i in enumerate(pieces)],
+            x=[to(hbase + i * w1, w1, None, 36 + j, mate) for j, i in enumerate((i1, c, d, e))])
 
     def ag_first(q, wide):
-        start(ag_copies(q, wide)['n1'])
+        cp = ag_copies(q, wide)
+        start(cp['n1'])
+        start(cp['n2'][0])
 
     def ag_fwd1(q, wide):
         cp = ag_copies(q, wide)
-        for a, b in zip(cp['n1'], cp['f1']):
-            a.wait_recv()
-            b.start()
+        for j in (0, 1):
+            cp['n1'][j].wait_recv()
+            cp['f1'][j].start()
+            start(cp['n2'][1 + j])
 
     def ag_second(q, wide):
         cp = ag_copies(q, wide)
         recv_wait(cp['f1'])
-        start(cp['n2'])
+        start(cp['n2'][3])
         if wide:
             pl.semaphore_wait(free.at[q], 1)
         cp['x'][0].start()
 
     def ag_fwd2(q, wide):
         cp = ag_copies(q, wide)
-        for a, b in zip(cp['n2'], cp['f2']):
+        for j in range(3):
+            for a, b in zip(cp['n2'][j], cp['f2'][j]):
+                a.wait_recv()
+                b.start()
+
+    def ag_fwd3(q, wide):
+        cp = ag_copies(q, wide)
+        for a, b in zip(cp['n2'][3], cp['f2'][3]):
             a.wait_recv()
             b.start()
         start(cp['x'][1:3])
 
     def ag_last(q, wide):
         cp = ag_copies(q, wide)
-        recv_wait(cp['f2'])
+        for pair in cp['f2']:
+            recv_wait(pair)
         cp['x'][3].start()
 
     def ag_mate(q, wide):
-        recv_wait(ag_copies(q, wide)['x'])
-
-    def partial_product(q, base):
-        v = lax.dot_general(dwt[...], xv[q, pl.ds(base, half), :], (((1,), (1,)), ((), ())),
-                            preferred_element_type=jnp.float32)
-        c_buf[q, :, pl.ds(base, half)] = v[:kf]
-
-    def gradient(q, base):
-        gacc[...] += jnp.dot(rt[q, :, pl.ds(base, half)], xv[q, pl.ds(base, half), :],
-                             preferred_element_type=jnp.float32)
+        recv_wait(ag_copies(q, wide)['x'][:3])
+
+    def ag_mate2(q, wide):
+        recv_wait(ag_copies(q, wide)['x'][3:])
+
+    def partial_product(q, base, js):
+        for j in js:
+            at = pl.ds(pl.multiple_of(base + blocks(q)[j] * w1, w1), w1)
+            v = lax.dot_general(dwt[...], xv[q, at, :], (((1,), (1,)), ((), ())), preferred_element_type=jnp.float32)
+            c_buf[q, :, at] = v[:kf]
+
+    def gradient(q, base, js):
+        total = None
+        for j in js:
+            at = pl.ds(pl.multiple_of(base + blocks(q)[j] * w1, w1), w1)
+            v = jnp.dot(rt[q, :, at], xv[q, at, :], preferred_element_type=jnp.float32)
+            total = v if total is None else total + v
+        gacc[...] += total
 
     def sweep(t, carry):
         first = t == 0
@@ -247,18 +275,23 @@
             def _():
                 f(q, True)
 
-        def product(q, mates):
-            @pl.when(first)
-            def _():
-                load_wait(q, peer if mates else core, pbase if mates else hbase)
-            partial_product(q, pbase if mates else hbase)
+        def product(q, mates, js, opens=False):
+            if opens:
+                @pl.when(first)
+                def _():
+                    load_wait(q, peer, pbase)
+                    load_wait(q, core, hbase)
+            partial_product(q, pbase if mates else hbase, js)
             if mates:
-                c_d2d(q).start()
-
-        def pair_sum(q):
-            c_d2d(q).wait_recv()
-            d_buf[q] = d_buf[q] + c_buf[q, :, pl.ds(hbase, half)]
-            rs_first(q, 0)
+                start([c_d2d(q, j) for j in js])
+
+        def pair_sum(q, js, then):
+            for j in js:
+                c_d2d(q, j).wait_recv()
+                at = blocks(q)[j] * w1
+                d_buf[q, :, lanes(at, w1)] = d_buf[q, :, lanes(at, w1)] + c_buf[q, :, lanes(hbase + at, w1)]
+            if then:
+                start(rs_copies(q, 0)[then])
 
         def sent(q, stage):
             cp = rs_copies(q, stage)
@@ -267,8 +300,9 @@
 
         def ring_sum(q):
             t_buf[q] = rs_total(q, 0)
-            rs_first(q, 1)
-            c_d2d(q).wait_send()
+            start(rs_copies(q, 1)['far'])
+            start(rs_copies(q, 1)['plain'])
+            send_wait([c_d2d(q, j) for j in range(4)])
 
             @pl.when(t == last)
             def _():
@@ -290,87 +324,46 @@
                 c_buf[q, :, at] = own[q, pl.ds(0, kf), :]
             gathers(ag_first, q)
 
-        product(0, True)
-        product(0, False)
-        product(1, True)
-        pair_sum(0)
-        product(1, False)
-        pair_sum(1)
-        product(2, True)
-        product(2, False)
-        rs_mid(0, 0)
-        product(3, True)
-        rs_mid(1, 0)
-        product(3, False)
-        pair_sum(2)
-        pair_sum(3)
-        ring_sum(0)
-        ring_sum(1)
-        rs_mid(0, 1)
-        rs_mid(1, 1)
-        rs_mid(2, 0)
-        rs_mid(3, 0)
-        finish(0)
-        finish(1)
-        gathers(ag_fwd1, 0)
-        gathers(ag_fwd1, 1)
-        ring_sum(2)
-        ring_sum(3)
-        gathers(ag_second, 0)
-        gathers(ag_second, 1)
-        rs_mid(2, 1)
-        rs_mid(3, 1)
-        gathers(ag_fwd2, 0)
-        gathers(ag_fwd2, 1)
-        finish(2)
-        finish(3)
-        gathers(ag_fwd1, 2)
-        gathers(ag_fwd1, 3)
-        gathers(ag_last, 0)
-        gathers(ag_last, 1)
-        gathers(ag_second, 2)
-        gathers(ag_second, 3)
+        def grad(q, base, js):
+            @pl.when(t < last)
+            def _():
+                gradient(q, base, js)
+
+        def drain(q, wide):
+            cp = ag_copies(q, wide)
+            for key in ('n1', 'f1', 'x'):
+                send_wait(cp[key])
+            for pair in cp['n2'] + cp['f2']:
+                send_wait(pair)
+
+        def drained(q):
+            sent(q, 1)
+            gathers(drain, q)
+
+        acts = {
+            'A': lambda q: product(q, True, (0,), True), 'B': lambda q: product(q, False, (0,)),
+            'P': lambda q: product(q, True, (1, 2)), 'O': lambda q: product(q, False, (1, 2)),
+            'p': lambda q: product(q, True, (3,)), 'o': lambda q: product(q, False, (3,)),
+            'S': lambda q: pair_sum(q, (0,), 'far'), 'N': lambda q: pair_sum(q, (1, 2), 'plain'),
+            's': lambda q: pair_sum(q, (3,), None),
+            'a': lambda q: rs_mid(q, 0), 'T': ring_sum, 'b': lambda q: rs_mid(q, 1), 'F': finish,
+            'c': lambda q: gathers(ag_fwd1, q), 'd': lambda q: gathers(ag_second, q),
+            'e': lambda q: gathers(ag_fwd2, q), 'k': lambda q: gathers(ag_fwd3, q), 'f': lambda q: gathers(ag_last, q),
+            'm': lambda q: gathers(ag_mate, q), 'n': lambda q: gathers(ag_mate2, q),
+            'G': lambda q: grad(q, hbase, (1, 2, 3)), 'g': lambda q: grad(q, hbase, (0,)),
+            'H': lambda q: grad(q, pbase, (1, 2, 3)), 'h': lambda q: grad(q, pbase, (0,)),
+            'D': drained,
+        }
+        for act in ' '.join(SCHEDULE).split():
+            with jax.named_scope(act):
+                acts[act[0]](int(act[1:]))
 
         @pl.when(t < last)
         def _():
-            gacc[...] = jnp.zeros_like(gacc)
-            gradient(0, hbase)
-            gradient(1, hbase)
-        gathers(ag_mate, 0)
-        gathers(ag_mate, 1)
-        gathers(ag_fwd2, 2)
-        gathers(ag_fwd2, 3)
-
-        @pl.when(t < last)
-        def _():
-            gradient(0, pbase)
-            gradient(1, pbase)
-        gathers(ag_last, 2)
-        gathers(ag_last, 3)
-
-        @pl.when(t < last)
-        def _():
-            gradient(2, hbase)
-            gradient(3, hbase)
-        gathers(ag_mate, 2)
-        gathers(ag_mate, 3)
-
-        def drain(q, wide):
-            cp = ag_copies(q, wide)
-            for key in ('n1', 'f1', 'n2', 'f2', 'x'):
-                send_wait(cp[key])
-
-        for q in range(q_all):
-            sent(q, 1)
-            gathers(drain, q)
-
-        @pl.when(t < last)
-        def _():
-            gradient(2, pbase)
-            gradient(3, pbase)
             update = eta_ref[...] * (gacc[...] * (1.0 / n) - (RIDGE_COEF / n) * w_ref[...])
             w_ref[...] = w_ref[...] + MIX_WEIGHT * update
             dwt[...] = update.astype(jnp.bfloat16)
+            gacc[...] = jnp.zeros_like(gacc)
         return carry
 
     lax.fori_loop(0, last + 1, sweep, 0)
@@ -427,8 +420,8 @@
                 pltpu.VMEM((CHUNKS, kb, w2), f32),
                 pltpu.VMEM((kb, feats), f32),
                 pltpu.VMEM((kb, feats), bf16),
-                pltpu.SemaphoreType.DMA((CHUNKS, 25)),
-                pltpu.SemaphoreType.DMA((CHUNKS, 25)),
+                pltpu.SemaphoreType.DMA((CHUNKS, 40)),
+                pltpu.SemaphoreType.DMA((CHUNKS, 40)),
                 pltpu.SemaphoreType.DMA((CHUNKS, CORES)),
                 pltpu.SemaphoreType.DMA,
                 pltpu.SemaphoreType.REGULAR((CHUNKS,)),

time: 424 us -> 353 us (0.83)
  Pallas kernels: 411 us -> 340 us
    pallas_call x1, Pallas kernels: 411 us -> 340 us  [local_solve(): pl.pallas_call(functools.partial(_kernel, n, side, kf, kb), out_shape=(ja...]
where the time goes in v2:
time: 353 us
  Pallas kernels  340 us (96%)
  local copies, waits for them, and re-layouts  11.7 us (3%)
    pallas_call x1, Pallas kernels, local_solve(): pl.pallas_call(functools.partial(_kernel, n, side, kf, kb), out_shape=(ja...  340 us
    transpose x2, local copies, waits for them, and re-layouts, local_solve(): return (w_out[:k].T, r_out[:k].T)  8.11 us

profile of v2, /device:TPU:97, one launch (start us, length us, event | category | flops | bytes accessed | tf_op | source)
XLA Modules:
  0.0 352.8 jit_solution(2486338857681946036)
XLA Ops:
  0.6 1.0 constant_dynamic-slice_fusion
  1.6 0.1 reshape.7
  1.7 0.7 pad.8.y_ref
  2.4 1.8 pad.9.w0_ref
  4.2 340.5 %shard_map.59 = (f32[112,1024]{1,0:T(8,128)}, f32[104,16384]{1,0:T(8,128)}) custom-call(bf16[16384,1024]{1,0:T(8,128)(2,1)} %x_hbm.1, f32[4,112,128]{2,1,0:T(8,128)} %pad.8.y_ref, f32[112,1024]{1,0:T(8,128)} %pad.9.w0_ref, f32[1,1024]{1,0:T(1,128)} %bitcast.13), custom_call_target="tpu_custom_call" | custom-call | tf_op jit(solution)/shard_map/pallas_call | solution.py:405
  344.7 1.8 slice_bitcast_fusion.1
  346.5 6.3 %slice_bitcast_fusion = f32[16384,100]{0,1:T(8,128)} fusion(f32[104,16384]{1,0:T(8,128)} %get-tuple-element.5), kind=kLoop, calls=%fused_computation | loop fusion | bytes 13107200 | tf_op jit(solution)/shard_map/transpose | solution.py:432
  (1 shorter events, 0.0 us)

commit v3 on v2

v3 whole, which is shorter than its diff:
```python
import functools
import math

import jax
import jax.numpy as jnp
from jax import lax
from jax.experimental import pallas as pl
from jax.experimental.pallas import tpu as pltpu
from jax.sharding import PartitionSpec as P

SWEEPS = 6
RIDGE_COEF = 1.0
MIX_WEIGHT = 0.75
CHUNKS = 4
CORES = 2
SCHEDULE = (
    'A0 A1 B0 B1', 'S0 S1 P0 P1', 'O0 N0 O1 N1', 'a0 a1 A2 A3', 'B2 B3 P2 S2', 'S3 P3 O2 N2', 'O3 N3 p0 p1',
    'o0 o1 s0 s1', 'T0 T1 p2 p3', 'a2 a3 o2 o3', 's2 s3 F0 F1', 'T2 T3 c0 c1', 'F2 F3 e0 e1', 'm0 m1 c2 c3',
    'Q01 H01 G01 n0', 'n1 h01 m2 m3', 'Q23 H23 e2 e3', 'G23 D0 D1 D2', 'D3 n2 n3 h23',
)
MESH = pl.DeviceIdType.MESH


class _Copy:
    def __init__(self, *args):
        self.args = args

    def _make(self):
        src, dst, send_sem, recv_sem, device = self.args
        return pltpu.make_async_remote_copy(src_ref=src, dst_ref=dst, send_sem=send_sem, recv_sem=recv_sem,
                                            device_id=device, device_id_type=MESH)

    def start(self):
        self._make().start()

    def wait_recv(self):
        self._make().wait_recv()

    def wait_send(self):
        self._make().wait_send()


def _up(v, m):
    return (v + m - 1) // m * m


def _split(v, m):
    top = _up(v // 2, m)
    return top, v - top


def _kernel(n, side, kf, kb, x_hbm, y_ref, w0_ref, eta_ref, w_ref, r_hbm,
            xv, c_buf, d_buf, far1, near1, near2, t_buf, rt, own, gacc, dwt,
            send, recv, load_sem, out_sem, free):
    q_all = CHUNKS
    rows = n // q_all
    half = rows // CORES
    w1 = half // side
    w2 = w1 // side
    ka, kc = _split(kf, 8)
    last = SWEEPS

    me = lax.axis_index('feat')
    core = lax.rem(me, CORES)
    px = lax.rem(me // CORES, side)
    py = me // (CORES * side)
    peer = 1 - core
    hbase = pl.multiple_of(core * half, half)
    pbase = pl.multiple_of(peer * half, half)

    def dev(yy, xx, cc):
        return {'feat': (yy * side + xx) * CORES + cc}

    def step(v, s):
        return lax.rem(v + (s + side), side)

    xp, xm = dev(py, step(px, 1), core), dev(py, step(px, -1), core)
    yp, ym = dev(step(py, 1), px, core), dev(step(py, -1), px, core)
    xf, yf = dev(py, step(px, 2), core), dev(step(py, 2), px, core)
    mate = dev(py, px, peer)
    ring_x, ring_y = (px, xp, xm, xf), (py, yp, ym, yf)
    rings = [(ring_x, ring_y) if q % 2 == 0 else (ring_y, ring_x) for q in range(q_all)]

    barrier = pltpu.get_barrier_semaphore()
    for d in (xp, xm, xf, yp, ym, yf, mate):
        pl.semaphore_signal(barrier, inc=1, device_id=d, device_id_type=MESH)

    def load(q, cc):
        def one(i, carry):
            a, b = i // side, lax.rem(i, side)
            d = ((b * side + a) if q % 2 == 0 else (a * side + b)) * CORES + cc
            src = x_hbm.at[pl.ds(pl.multiple_of(d * (q_all * w2) + q * w2, w2), w2), :]
            dst = xv.at[q, pl.ds(pl.multiple_of(cc * half + i * w2, w2), w2), :]
            pltpu.make_async_copy(src, dst, load_sem.at[q, cc]).start()
            return carry
        lax.fori_loop(0, side * side, one, 0)

    def load_wait(q, cc, base):
        ref = xv.at[q, pl.ds(base, half), :]
        pltpu.make_async_copy(ref, ref, load_sem.at[q, cc]).wait()

    for q in range(q_all):
        load(q, peer)
        load(q, core)

    own[...] = y_ref[...]
    gacc[...] = jnp.zeros_like(gacc)
    w_ref[...] = w0_ref[...]
    dwt[...] = w0_ref[...].astype(jnp.bfloat16)
    pl.semaphore_wait(barrier, 7)

    def rc(src, dst, q, k, device):
        return _Copy(src, dst, send.at[q, k], recv.at[q, k], device)

    def lanes(base, width):
        return pl.ds(pl.multiple_of(base, 128), width)

    def blocks(q):
        idx = rings[q][0][0]
        return step(idx, 2), step(idx, 1), step(idx, -1), idx

    def c_d2d(q, j):
        at = blocks(q)[j] * w1
        return rc(c_buf.at[q, :, lanes(pbase + at, w1)], d_buf.at[q, :, lanes(at, w1)], q, j, mate)

    def ring_copies(q):
        idx, plus, minus, _ = rings[q][0]

        def cut(i, lo, size):
            return d_buf.at[q, pl.ds(lo, size), lanes(i * w1, w1)]

        f, p, m = step(idx, 2), step(idx, 1), step(idx, -1)
        return dict(
            far=(rc(cut(f, 0, ka), far1.at[q, 0], q, 4, plus),
                 rc(cut(f, ka, kc), far1.at[q, 1, pl.ds(0, kc), :], q, 5, minus)),
            plain=(rc(cut(p, ka, kc), near1.at[q, 0, pl.ds(ka, kc), :], q, 6, plus),
                   rc(cut(m, 0, ka), near1.at[q, 1, pl.ds(0, ka), :], q, 7, minus)),
            aug=(rc(cut(p, 0, ka), near1.at[q, 0, pl.ds(0, ka), :], q, 8, plus),
                 rc(cut(m, ka, kc), near1.at[q, 1, pl.ds(ka, kc), :], q, 9, minus)))

    def direct_copies(q):
        idx, plus, minus, far = rings[q][1]
        return [rc(t_buf.at[q, :, lanes(step(idx, s) * w2, w2)], near2.at[q, j], q, 10 + j, device)
                for j, (s, device) in enumerate(((2, far), (1, plus), (-1, minus)))]

    def start(copies):
        for c in copies:
            c.start()

    def recv_wait(copies):
        for c in copies:
            c.wait_recv()

    def send_wait(copies):
        for c in copies:
            c.wait_send()

    def ring_mid(q):
        idx = rings[q][0][0]
        cp = ring_copies(q)
        p, m = step(idx, 1), step(idx, -1)
        cp['far'][0].wait_recv()
        at = (q, pl.ds(0, ka), lanes(p * w1, w1))
        d_buf[at] = d_buf[at] + far1[q, 0]
        cp['aug'][0].start()
        cp['far'][1].wait_recv()
        at = (q, pl.ds(ka, kc), lanes(m * w1, w1))
        d_buf[at] = d_buf[at] + far1[q, 1, pl.ds(0, kc), :]
        cp['aug'][1].start()

    def ring_total(q):
        cp = ring_copies(q)
        recv_wait(cp['plain'])
        recv_wait(cp['aug'])
        return d_buf[q, :, lanes(rings[q][0][0] * w1, w1)] + (near1[q, 0] + near1[q, 1])

    def direct_total(q):
        recv_wait(direct_copies(q))
        return t_buf[q, :, lanes(rings[q][1][0] * w2, w2)] + near2[q, 0] + (near2[q, 1] + near2[q, 2])

    def ag_copies(q, wide):
        (i1, p1, m1, o1), (i2, p2, m2, o2) = rings[q]
        buf = c_buf if wide else rt
        b0 = hbase + i1 * w1

        def to(base, width, k, device):
            ref = buf.at[q, :, lanes(base, width)]
            return rc(ref, ref, q, k, device)

        pieces = [b0 + step(i2, s) * w2 for s in (0, -1, 1, 2)]
        return dict(
            n1=[to(pieces[0], w2, 13 + j, device) for j, device in enumerate((p2, m2, o2))],
            n2=[[to(at, w2, 16 + 3 * i + j, device) for j, device in enumerate((p1, m1, o1))]
                for i, at in enumerate(pieces)],
            x=[to(hbase + step(i1, s) * w1, w1, 28 + j, mate) for j, s in enumerate((0, -1, 1, 2))])

    def ag_first(q, wide):
        cp = ag_copies(q, wide)
        start(cp['n1'])
        start(cp['n2'][0])

    def ag_second(q, wide):
        cp = ag_copies(q, wide)
        for j in range(3):
            cp['n1'][j].wait_recv()
            start(cp['n2'][1 + j])
        if wide:
            pl.semaphore_wait(free.at[q], 1)
        cp['x'][0].start()

    def ag_third(q, wide):
        cp = ag_copies(q, wide)
        for j in range(3):
            for i in range(4):
                cp['n2'][i][j].wait_recv()
            cp['x'][1 + j].start()

    def ag_mate(q, wide):
        ag_copies(q, wide)['x'][0].wait_recv()

    def ag_mate2(q, wide):
        recv_wait(ag_copies(q, wide)['x'][1:])

    def partial_product(q, base, js):
        for j in js:
            at = pl.ds(pl.multiple_of(base + blocks(q)[j] * w1, w1), w1)
            v = lax.dot_general(dwt[...], xv[q, at, :], (((1,), (1,)), ((), ())), preferred_element_type=jnp.float32)
            c_buf[q, :, at] = v[:kf]

    def gradient(parts):
        total = None
        for q, base, j in parts:
            at = pl.ds(pl.multiple_of(base + blocks(q)[j] * w1, w1), w1)
            v = jnp.dot(rt[q, :, at], xv[q, at, :], preferred_element_type=jnp.float32)
            total = v if total is None else total + v
        gacc[...] += total

    def sweep(t, carry):
        first = t == 0
        scale = jnp.where(first, jnp.float32(1.0), jnp.float32(MIX_WEIGHT))

        def gathers(f, q):
            @pl.when(t < last)
            def _():
                f(q, False)

            @pl.when(t == last)
            def _():
                f(q, True)

        def product(q, mates, js, opens=False):
            if opens:
                @pl.when(first)
                def _():
                    load_wait(q, peer, pbase)
                    load_wait(q, core, hbase)
            partial_product(q, pbase if mates else hbase, js)
            if mates:
                start([c_d2d(q, j) for j in js])

        def pair_sum(q, js, then):
            for j in js:
                c_d2d(q, j).wait_recv()
                at = blocks(q)[j] * w1
                d_buf[q, :, lanes(at, w1)] = d_buf[q, :, lanes(at, w1)] + c_buf[q, :, lanes(hbase + at, w1)]
            if then:
                start(ring_copies(q)[then])

        def ring_sum(q):
            t_buf[q] = ring_total(q)
            start(direct_copies(q))
            send_wait([c_d2d(q, j) for j in range(4)])

            @pl.when(t == last)
            def _():
                pl.semaphore_signal(free.at[q], inc=1, device_id=mate, device_id_type=MESH)

        def finish(q):
            fresh = own[q, pl.ds(0, kf), :] - scale * direct_total(q)
            own[q, pl.ds(0, kf), :] = fresh
            for copies in ring_copies(q).values():
                send_wait(copies)
            idx = rings[q]
            at = lanes(hbase + idx[0][0] * w1 + idx[1][0] * w2, w2)

            @pl.when(t < last)
            def _():
                rt[q, :, at] = own[q].astype(jnp.bfloat16)

            @pl.when(t == last)
            def _():
                c_buf[q, :, at] = own[q, pl.ds(0, kf), :]
            gathers(ag_first, q)

        def grad(qs, base, js):
            @pl.when(t < last)
            def _():
                gradient([(q, base, j) for q in qs for j in js])

        def drain(q, wide):
            cp = ag_copies(q, wide)
            for copies in [cp['n1'], cp['x']] + cp['n2']:
                send_wait(copies)

        def drained(q):
            send_wait(direct_copies(q))
            gathers(drain, q)

        def each(f):
            return lambda qs: [f(q) for q in qs]

        acts = {
            'A': each(lambda q: product(q, True, (0,), True)), 'B': each(lambda q: product(q, False, (0,))),
            'P': each(lambda q: product(q, True, (1, 2))), 'O': each(lambda q: product(q, False, (1, 2))),
            'p': each(lambda q: product(q, True, (3,))), 'o': each(lambda q: product(q, False, (3,))),
            'S': each(lambda q: pair_sum(q, (0,), 'far')), 'N': each(lambda q: pair_sum(q, (1, 2), 'plain')),
            's': each(lambda q: pair_sum(q, (3,), None)),
            'a': each(ring_mid), 'T': each(ring_sum), 'F': each(finish),
            'c': each(lambda q: gathers(ag_second, q)), 'e': each(lambda q: gathers(ag_third, q)),
            'm': each(lambda q: gathers(ag_mate, q)), 'n': each(lambda q: gathers(ag_mate2, q)),
            'Q': lambda qs: grad(qs, hbase, (3,)), 'G': lambda qs: grad(qs, hbase, (0, 1, 2)),
            'H': lambda qs: grad(qs, pbase, (3,)), 'h': lambda qs: grad(qs, pbase, (0, 1, 2)),
            'D': each(drained),
        }
        for act in ' '.join(SCHEDULE).split():
            with jax.named_scope(act):
                acts[act[0]]([int(v) for v in act[1:]])

        @pl.when(t < last)
        def _():
            update = eta_ref[...] * (gacc[...] * (1.0 / n) - (RIDGE_COEF / n) * w_ref[...])
            w_ref[...] = w_ref[...] + MIX_WEIGHT * update
            dwt[...] = update.astype(jnp.bfloat16)
            gacc[...] = jnp.zeros_like(gacc)
        return carry

    lax.fori_loop(0, last + 1, sweep, 0)

    def piece(i, carry):
        for q in range(q_all):
            cc, j = i // (side * side), lax.rem(i, side * side)
            a, b = j // side, lax.rem(j, side)
            d = ((b * side + a) if q % 2 == 0 else (a * side + b)) * CORES + cc
            pltpu.make_async_copy(c_buf.at[q, :, lanes(i * w2, w2)],
                                  r_hbm.at[:, lanes((d * q_all + q) * w2, w2)], out_sem).start()
        return carry
    lax.fori_loop(0, CORES * side * side, piece, 0)
    for q in range(q_all):
        pltpu.make_async_copy(c_buf.at[q], c_buf.at[q], out_sem).wait()


def solution(mesh):
    group = mesh.shape['feat']
    side = math.isqrt(group // CORES)

    def local_solve(design, targets, weights, step_sizes):
        n, feats = design.shape
        k = targets.shape[1]
        kf, kb = _up(k, 8), _up(k, 16)
        rows = n // CHUNKS
        half = rows // CORES
        w1 = half // side
        w2 = w1 // side
        ka = _split(kf, 8)[0]
        share = n // group
        me = lax.axis_index('feat')
        mine = lax.dynamic_slice_in_dim(targets, me * share, share, 0)
        mine = jnp.pad(jnp.swapaxes(mine.reshape(CHUNKS, w2, k), 1, 2), ((0, 0), (0, kb - k), (0, 0)))
        wt = jnp.pad(weights.T, ((0, kb - k), (0, 0)))
        f32, bf16 = jnp.float32, jnp.bfloat16
        vm = pl.BlockSpec(memory_space=pltpu.VMEM)
        hb = pl.BlockSpec(memory_space=pl.ANY)
        w_out, r_out = pl.pallas_call(
            functools.partial(_kernel, n, side, kf, kb),
            out_shape=(jax.ShapeDtypeStruct((kb, feats), f32), jax.ShapeDtypeStruct((kf, n), f32)),
            in_specs=[hb, vm, vm, vm],
            out_specs=(vm, hb),
            scratch_shapes=[
                pltpu.VMEM((CHUNKS, rows, feats), bf16),
                pltpu.VMEM((CHUNKS, kf, rows), f32),
                pltpu.VMEM((CHUNKS, kf, half), f32),
                pltpu.VMEM((CHUNKS, 2, ka, w1), f32),
                pltpu.VMEM((CHUNKS, 2, kf, w1), f32),
                pltpu.VMEM((CHUNKS, 3, kf, w2), f32),
                pltpu.VMEM((CHUNKS, kf, w1), f32),
                pltpu.VMEM((CHUNKS, kb, rows), bf16),
                pltpu.VMEM((CHUNKS, kb, w2), f32),
                pltpu.VMEM((kb, feats), f32),
                pltpu.VMEM((kb, feats), bf16),
                pltpu.SemaphoreType.DMA((CHUNKS, 32)),
                pltpu.SemaphoreType.DMA((CHUNKS, 32)),
                pltpu.SemaphoreType.DMA((CHUNKS, CORES)),
                pltpu.SemaphoreType.DMA,
                pltpu.SemaphoreType.REGULAR((CHUNKS,)),
            ],
            compiler_params=pltpu.CompilerParams(
                collective_id=0, has_side_effects=True, vmem_limit_bytes=67043328),
        )(design, mine, wt, step_sizes[None, :])
        return w_out[:k].T, r_out[:k].T

    return jax.shard_map(
        local_solve,
        mesh=mesh,
        in_specs=(P('prob', 'feat'), P('prob', None), P(('prob', 'feat'), None), P(('prob', 'feat'))),
        out_specs=(P(('prob', 'feat'), None), P('prob', None)),
        check_vma=False,
    )
```

time: 353 us -> 328 us (0.929)
  Pallas kernels: 340 us -> 316 us
    pallas_call x1, Pallas kernels: 340 us -> 316 us  [local_solve(): pl.pallas_call(functools.partial(_kernel, n, side, kf, kb), out_shape=(ja...]
where the time goes in v3:
time: 328 us
  Pallas kernels  316 us (96%)
  local copies, waits for them, and re-layouts  11.7 us (4%)
    pallas_call x1, Pallas kernels, local_solve(): pl.pallas_call(functools.partial(_kernel, n, side, kf, kb), out_shape=(ja...  316 us
    transpose x2, local copies, waits for them, and re-layouts, local_solve(): return (w_out[:k].T, r_out[:k].T)  8.11 us

profile of v3, /device:TPU:97, one launch (start us, length us, event | category | flops | bytes accessed | tf_op | source)
XLA Modules:
  0.0 328.0 jit_solution(11411597535387546814)
XLA Ops:
  0.6 1.0 constant_dynamic-slice_fusion
  1.6 0.1 reshape.7
  1.7 0.7 pad.8.y_ref
  2.4 1.8 pad.9.w0_ref
  4.2 315.7 %shard_map.59 = (f32[112,1024]{1,0:T(8,128)}, f32[104,16384]{1,0:T(8,128)}) custom-call(bf16[16384,1024]{1,0:T(8,128)(2,1)} %x_hbm.1, f32[4,112,128]{2,1,0:T(8,128)} %pad.8.y_ref, f32[112,1024]{1,0:T(8,128)} %pad.9.w0_ref, f32[1,1024]{1,0:T(1,128)} %bitcast.13), custom_call_target="tpu_custom_call" | custom-call | tf_op jit(solution)/shard_map/pallas_call | solution.py:373
  319.9 1.8 slice_bitcast_fusion.1
  321.7 6.3 %slice_bitcast_fusion = f32[16384,100]{0,1:T(8,128)} fusion(f32[104,16384]{1,0:T(8,128)} %get-tuple-element.5), kind=kLoop, calls=%fused_computation | loop fusion | bytes 13107200 | tf_op jit(solution)/shard_map/transpose | solution.py:399
  (1 shorter events, 0.0 us)

commit v4 on v3

--- a/solution.py
+++ b/solution.py
@@ -16,7 +16,7 @@
 SCHEDULE = (
     'A0 A1 B0 B1', 'S0 S1 P0 P1', 'O0 N0 O1 N1', 'a0 a1 A2 A3', 'B2 B3 P2 S2', 'S3 P3 O2 N2', 'O3 N3 p0 p1',
     'o0 o1 s0 s1', 'T0 T1 p2 p3', 'a2 a3 o2 o3', 's2 s3 F0 F1', 'T2 T3 c0 c1', 'F2 F3 e0 e1', 'm0 m1 c2 c3',
-    'Q01 H01 G01 n0', 'n1 h01 m2 m3', 'Q23 H23 e2 e3', 'G23 D0 D1 D2', 'D3 n2 n3 h23',
+    'Q01 H01 G01 n0', 'n1 R0 R1 h01', 'm2 m3 Q23 H23', 'e2 e3 G23 D0', 'D1 D2 D3 n2', 'n3 R2 R3 h23',
 )
 MESH = pl.DeviceIdType.MESH
 
@@ -40,24 +40,16 @@
         self._make().wait_send()
 
 
-def _up(v, m):
-    return (v + m - 1) // m * m
-
-
-def _split(v, m):
-    top = _up(v // 2, m)
-    return top, v - top
-
-
-def _kernel(n, side, kf, kb, x_hbm, y_ref, w0_ref, eta_ref, w_ref, r_hbm,
-            xv, c_buf, d_buf, far1, near1, near2, t_buf, rt, own, gacc, dwt,
+def _kernel(n, side, x_hbm, y_hbm, w0_ref, eta_ref, w_ref, r_hbm,
+            xv, c_buf, d_buf, far1, near1, near2, t_buf, rt, own, gacc, dwt, y_own,
             send, recv, load_sem, out_sem, free):
     q_all = CHUNKS
     rows = n // q_all
     half = rows // CORES
     w1 = half // side
     w2 = w1 // side
-    ka, kc = _split(kf, 8)
+    wh = w1 // 2
+    share = q_all * w2
     last = SWEEPS
 
     me = lax.axis_index('feat')
@@ -99,14 +91,18 @@
         ref = xv.at[q, pl.ds(base, half), :]
         pltpu.make_async_copy(ref, ref, load_sem.at[q, cc]).wait()
 
+    targets_in = pltpu.make_async_copy(y_hbm.at[:, pl.ds(pl.multiple_of(me * share, share), share)], y_own, out_sem)
+    targets_in.start()
     for q in range(q_all):
         load(q, peer)
         load(q, core)
 
-    own[...] = y_ref[...]
     gacc[...] = jnp.zeros_like(gacc)
     w_ref[...] = w0_ref[...]
     dwt[...] = w0_ref[...].astype(jnp.bfloat16)
+    targets_in.wait()
+    for q in range(q_all):
+        own[q] = y_own[:, q * w2:(q + 1) * w2]
     pl.semaphore_wait(barrier, 7)
 
     def rc(src, dst, q, k, device):
@@ -126,17 +122,17 @@
     def ring_copies(q):
         idx, plus, minus, _ = rings[q][0]
 
-        def cut(i, lo, size):
-            return d_buf.at[q, pl.ds(lo, size), lanes(i * w1, w1)]
+        def cut(i, side_half):
+            return d_buf.at[q, :, lanes(i * w1 + side_half * wh, wh)]
+
+        def into(j, side_half):
+            return near1.at[q, j, :, pl.ds(side_half * wh, wh)]
 
         f, p, m = step(idx, 2), step(idx, 1), step(idx, -1)
         return dict(
-            far=(rc(cut(f, 0, ka), far1.at[q, 0], q, 4, plus),
-                 rc(cut(f, ka, kc), far1.at[q, 1, pl.ds(0, kc), :], q, 5, minus)),
-            plain=(rc(cut(p, ka, kc), near1.at[q, 0, pl.ds(ka, kc), :], q, 6, plus),
-                   rc(cut(m, 0, ka), near1.at[q, 1, pl.ds(0, ka), :], q, 7, minus)),
-            aug=(rc(cut(p, 0, ka), near1.at[q, 0, pl.ds(0, ka), :], q, 8, plus),
-                 rc(cut(m, ka, kc), near1.at[q, 1, pl.ds(ka, kc), :], q, 9, minus)))
+            far=(rc(cut(f, 0), far1.at[q, 0], q, 4, plus), rc(cut(f, 1), far1.at[q, 1], q, 5, minus)),
+            plain=(rc(cut(p, 1), into(0, 1), q, 6, plus), rc(cut(m, 0), into(1, 0), q, 7, minus)),
+            aug=(rc(cut(p, 0), into(0, 0), q, 8, plus), rc(cut(m, 1), into(1, 1), q, 9, minus)))
 
     def direct_copies(q):
         idx, plus, minus, far = rings[q][1]
@@ -159,14 +155,11 @@
         idx = rings[q][0][0]
         cp = ring_copies(q)
         p, m = step(idx, 1), step(idx, -1)
-        cp['far'][0].wait_recv()
-        at = (q, pl.ds(0, ka), lanes(p * w1, w1))
-        d_buf[at] = d_buf[at] + far1[q, 0]
-        cp['aug'][0].start()
-        cp['far'][1].wait_recv()
-        at = (q, pl.ds(ka, kc), lanes(m * w1, w1))
-        d_buf[at] = d_buf[at] + far1[q, 1, pl.ds(0, kc), :]
-        cp['aug'][1].start()
+        for j, i in enumerate((p, m)):
+            cp['far'][j].wait_recv()
+            at = (q, slice(None), lanes(i * w1 + j * wh, wh))
+            d_buf[at] = d_buf[at] + far1[q, j]
+            cp['aug'][j].start()
 
     def ring_total(q):
         cp = ring_copies(q)
@@ -225,7 +218,7 @@
         for j in js:
             at = pl.ds(pl.multiple_of(base + blocks(q)[j] * w1, w1), w1)
             v = lax.dot_general(dwt[...], xv[q, at, :], (((1,), (1,)), ((), ())), preferred_element_type=jnp.float32)
-            c_buf[q, :, at] = v[:kf]
+            c_buf[q, :, at] = v
 
     def gradient(parts):
         total = None
@@ -276,8 +269,8 @@
                 pl.semaphore_signal(free.at[q], inc=1, device_id=mate, device_id_type=MESH)
 
         def finish(q):
-            fresh = own[q, pl.ds(0, kf), :] - scale * direct_total(q)
-            own[q, pl.ds(0, kf), :] = fresh
+            fresh = own[q] - scale * direct_total(q)
+            own[q] = fresh
             for copies in ring_copies(q).values():
                 send_wait(copies)
             idx = rings[q]
@@ -289,7 +282,7 @@
 
             @pl.when(t == last)
             def _():
-                c_buf[q, :, at] = own[q, pl.ds(0, kf), :]
+                c_buf[q, :, at] = own[q]
             gathers(ag_first, q)
 
         def grad(qs, base, js):
@@ -305,6 +298,19 @@
         def drained(q):
             send_wait(direct_copies(q))
             gathers(drain, q)
+
+        def put(q):
+            def piece(i, carry):
+                cc, j = i // (side * side), lax.rem(i, side * side)
+                a, b = j // side, lax.rem(j, side)
+                d = ((b * side + a) if q % 2 == 0 else (a * side + b)) * CORES + cc
+                pltpu.make_async_copy(c_buf.at[q, :, lanes(i * w2, w2)],
+                                      r_hbm.at[:, lanes((d * q_all + q) * w2, w2)], out_sem).start()
+                return carry
+
+            @pl.when(t == last)
+            def _():
+                lax.fori_loop(0, CORES * side * side, piece, 0)
 
         def each(f):
             return lambda qs: [f(q) for q in qs]
@@ -320,7 +326,7 @@
             'm': each(lambda q: gathers(ag_mate, q)), 'n': each(lambda q: gathers(ag_mate2, q)),
             'Q': lambda qs: grad(qs, hbase, (3,)), 'G': lambda qs: grad(qs, hbase, (0, 1, 2)),
             'H': lambda qs: grad(qs, pbase, (3,)), 'h': lambda qs: grad(qs, pbase, (0, 1, 2)),
-            'D': each(drained),
+            'D': each(drained), 'R': each(put),
         }
         for act in ' '.join(SCHEDULE).split():
             with jax.named_scope(act):
@@ -336,15 +342,6 @@
 
     lax.fori_loop(0, last + 1, sweep, 0)
 
-    def piece(i, carry):
-        for q in range(q_all):
-            cc, j = i // (side * side), lax.rem(i, side * side)
-            a, b = j // side, lax.rem(j, side)
-            d = ((b * side + a) if q % 2 == 0 else (a * side + b)) * CORES + cc
-            pltpu.make_async_copy(c_buf.at[q, :, lanes(i * w2, w2)],
-                                  r_hbm.at[:, lanes((d * q_all + q) * w2, w2)], out_sem).start()
-        return carry
-    lax.fori_loop(0, CORES * side * side, piece, 0)
     for q in range(q_all):
         pltpu.make_async_copy(c_buf.at[q], c_buf.at[q], out_sem).wait()
 
@@ -356,37 +353,31 @@
     def local_solve(design, targets, weights, step_sizes):
         n, feats = design.shape
         k = targets.shape[1]
-        kf, kb = _up(k, 8), _up(k, 16)
         rows = n // CHUNKS
         half = rows // CORES
         w1 = half // side
         w2 = w1 // side
-        ka = _split(kf, 8)[0]
-        share = n // group
-        me = lax.axis_index('feat')
-        mine = lax.dynamic_slice_in_dim(targets, me * share, share, 0)
-        mine = jnp.pad(jnp.swapaxes(mine.reshape(CHUNKS, w2, k), 1, 2), ((0, 0), (0, kb - k), (0, 0)))
-        wt = jnp.pad(weights.T, ((0, kb - k), (0, 0)))
         f32, bf16 = jnp.float32, jnp.bfloat16
         vm = pl.BlockSpec(memory_space=pltpu.VMEM)
         hb = pl.BlockSpec(memory_space=pl.ANY)
         w_out, r_out = pl.pallas_call(
-            functools.partial(_kernel, n, side, kf, kb),
-            out_shape=(jax.ShapeDtypeStruct((kb, feats), f32), jax.ShapeDtypeStruct((kf, n), f32)),
-            in_specs=[hb, vm, vm, vm],
+            functools.partial(_kernel, n, side),
+            out_shape=(jax.ShapeDtypeStruct((k, feats), f32), jax.ShapeDtypeStruct((k, n), f32)),
+            in_specs=[hb, hb, vm, vm],
             out_specs=(vm, hb),
             scratch_shapes=[
                 pltpu.VMEM((CHUNKS, rows, feats), bf16),
-                pltpu.VMEM((CHUNKS, kf, rows), f32),
-                pltpu.VMEM((CHUNKS, kf, half), f32),
-                pltpu.VMEM((CHUNKS, 2, ka, w1), f32),
-                pltpu.VMEM((CHUNKS, 2, kf, w1), f32),
-                pltpu.VMEM((CHUNKS, 3, kf, w2), f32),
-                pltpu.VMEM((CHUNKS, kf, w1), f32),
-                pltpu.VMEM((CHUNKS, kb, rows), bf16),
-                pltpu.VMEM((CHUNKS, kb, w2), f32),
-                pltpu.VMEM((kb, feats), f32),
-                pltpu.VMEM((kb, feats), bf16),
+                pltpu.VMEM((CHUNKS, k, rows), f32),
+                pltpu.VMEM((CHUNKS, k, half), f32),
+                pltpu.VMEM((CHUNKS, 2, k, w1 // 2), f32),
+                pltpu.VMEM((CHUNKS, 2, k, w1), f32),
+                pltpu.VMEM((CHUNKS, 3, k, w2), f32),
+                pltpu.VMEM((CHUNKS, k, w1), f32),
+                pltpu.VMEM((CHUNKS, k, rows), bf16),
+                pltpu.VMEM((CHUNKS, k, w2), f32),
+                pltpu.VMEM((k, feats), f32),
+                pltpu.VMEM((k, feats), bf16),
+                pltpu.VMEM((k, CHUNKS * w2), f32),
                 pltpu.SemaphoreType.DMA((CHUNKS, 32)),
                 pltpu.SemaphoreType.DMA((CHUNKS, 32)),
                 pltpu.SemaphoreType.DMA((CHUNKS, CORES)),
@@ -395,8 +386,8 @@
             ],
             compiler_params=pltpu.CompilerParams(
                 collective_id=0, has_side_effects=True, vmem_limit_bytes=67043328),
-        )(design, mine, wt, step_sizes[None, :])
-        return w_out[:k].T, r_out[:k].T
+        )(design, targets.T, weights.T, step_sizes[None, :])
+        return w_out.T, r_out.T
 
     return jax.shard_map(
         local_solve,

time: 328 us -> 316 us (0.963)
  Pallas kernels: 316 us -> 307 us
  local copies, waits for them, and re-layouts: 11.7 us -> 8.11 us
    pallas_call x1, Pallas kernels: 316 us -> 307 us  [local_solve(): pl.pallas_call(functools.partial(_kernel, n, side), out_shape=(jax.ShapeD...]
    transpose x2 -> x0, local copies, waits for them, and re-layouts: 8.11 us -> none  [local_solve(): return (w_out[:k].T, r_out[:k].T)]
    unnamed x0 -> x2, local copies, waits for them, and re-layouts: none -> 8.11 us
where the time goes in v4:
time: 316 us
  Pallas kernels  307 us (97%)
  local copies, waits for them, and re-layouts  8.11 us (3%)
    pallas_call x1, Pallas kernels, local_solve(): pl.pallas_call(functools.partial(_kernel, n, side), out_shape=(jax.ShapeD...  307 us
    unnamed x2, local copies, waits for them, and re-layouts  8.11 us

profile of v4, /device:TPU:97, one launch (start us, length us, event | category | flops | bytes accessed | tf_op | source)
XLA Modules:
  0.0 315.8 jit_solution(4379743326666630258)
XLA Ops:
  0.6 307.0 %shard_map.59 = (f32[100,1024]{1,0:T(8,128)}, f32[100,16384]{1,0:T(8,128)}) custom-call(bf16[16384,1024]{1,0:T(8,128)(2,1)} %x_hbm.1, f32[100,16384]{1,0:T(8,128)} %bitcast.5, f32[100,1024]{1,0:T(8,128)} %bitcast.7, f32[1,1024]{1,0:T(1,128)} %bitcast.9), custom_call_target="tpu_custom_call" | custom-call | tf_op jit(solution)/shard_map/pallas_call | solution.py:363
  307.7 1.8 copy.8
  309.5 6.3 %copy.9 = f32[16384,100]{0,1:T(8,128)} copy(f32[16384,100]{0,1:T(8,128)} %bitcast.6) | data formatting | bytes 13107200

commit v5 on v4

--- a/solution.py
+++ b/solution.py
@@ -13,6 +13,7 @@
 MIX_WEIGHT = 0.75
 CHUNKS = 4
 CORES = 2
+PARTS = 8
 SCHEDULE = (
     'A0 A1 B0 B1', 'S0 S1 P0 P1', 'O0 N0 O1 N1', 'a0 a1 A2 A3', 'B2 B3 P2 S2', 'S3 P3 O2 N2', 'O3 N3 p0 p1',
     'o0 o1 s0 s1', 'T0 T1 p2 p3', 'a2 a3 o2 o3', 's2 s3 F0 F1', 'T2 T3 c0 c1', 'F2 F3 e0 e1', 'm0 m1 c2 c3',
@@ -77,25 +78,35 @@
     for d in (xp, xm, xf, yp, ym, yf, mate):
         pl.semaphore_signal(barrier, inc=1, device_id=d, device_id_type=MESH)
 
-    def load(q, cc):
-        def one(i, carry):
-            a, b = i // side, lax.rem(i, side)
+    def blocks(q):
+        idx = rings[q][0][0]
+        return step(idx, 2), step(idx, 1), step(idx, -1), idx
+
+    def load(q, cc, j):
+        a = blocks(q)[j]
+
+        def one(b, carry):
             d = ((b * side + a) if q % 2 == 0 else (a * side + b)) * CORES + cc
-            src = x_hbm.at[pl.ds(pl.multiple_of(d * (q_all * w2) + q * w2, w2), w2), :]
-            dst = xv.at[q, pl.ds(pl.multiple_of(cc * half + i * w2, w2), w2), :]
-            pltpu.make_async_copy(src, dst, load_sem.at[q, cc]).start()
+            src = x_hbm.at[pl.ds(pl.multiple_of(d * share + q * w2, w2), w2), :]
+            dst = xv.at[q, pl.ds(pl.multiple_of(cc * half + a * w1 + b * w2, w2), w2), :]
+            pltpu.make_async_copy(src, dst, load_sem.at[q, cc, j]).start()
             return carry
-        lax.fori_loop(0, side * side, one, 0)
-
-    def load_wait(q, cc, base):
-        ref = xv.at[q, pl.ds(base, half), :]
-        pltpu.make_async_copy(ref, ref, load_sem.at[q, cc]).wait()
+        lax.fori_loop(0, side, one, 0)
+
+    def load_wait(q, js):
+        for cc in (peer, core):
+            for j in js:
+                ref = xv.at[q, pl.ds(pl.multiple_of(cc * half + blocks(q)[j] * w1, w1), w1), :]
+                pltpu.make_async_copy(ref, ref, load_sem.at[q, cc, j]).wait()
 
     targets_in = pltpu.make_async_copy(y_hbm.at[:, pl.ds(pl.multiple_of(me * share, share), share)], y_own, out_sem)
     targets_in.start()
-    for q in range(q_all):
-        load(q, peer)
-        load(q, core)
+    for qs in ((0, 1), (2, 3)):
+        for js in ((0,), (1, 2), (3,)):
+            for q in qs:
+                for cc in (peer, core):
+                    for j in js:
+                        load(q, cc, j)
 
     gacc[...] = jnp.zeros_like(gacc)
     w_ref[...] = w0_ref[...]
@@ -110,10 +121,6 @@
 
     def lanes(base, width):
         return pl.ds(pl.multiple_of(base, 128), width)
-
-    def blocks(q):
-        idx = rings[q][0][0]
-        return step(idx, 2), step(idx, 1), step(idx, -1), idx
 
     def c_d2d(q, j):
         at = blocks(q)[j] * w1
@@ -241,12 +248,11 @@
             def _():
                 f(q, True)
 
-        def product(q, mates, js, opens=False):
-            if opens:
+        def product(q, mates, js):
+            if mates and (q < 2 or 0 in js):
                 @pl.when(first)
                 def _():
-                    load_wait(q, peer, pbase)
-                    load_wait(q, core, hbase)
+                    load_wait(q, js if q < 2 else range(4))
             partial_product(q, pbase if mates else hbase, js)
             if mates:
                 start([c_d2d(q, j) for j in js])
@@ -316,7 +322,7 @@
             return lambda qs: [f(q) for q in qs]
 
         acts = {
-            'A': each(lambda q: product(q, True, (0,), True)), 'B': each(lambda q: product(q, False, (0,))),
+            'A': each(lambda q: product(q, True, (0,))), 'B': each(lambda q: product(q, False, (0,))),
             'P': each(lambda q: product(q, True, (1, 2))), 'O': each(lambda q: product(q, False, (1, 2))),
             'p': each(lambda q: product(q, True, (3,))), 'o': each(lambda q: product(q, False, (3,))),
             'S': each(lambda q: pair_sum(q, (0,), 'far')), 'N': each(lambda q: pair_sum(q, (1, 2), 'plain')),
@@ -344,6 +350,27 @@
 
     for q in range(q_all):
         pltpu.make_async_copy(c_buf.at[q], c_buf.at[q], out_sem).wait()
+
+
+def _store(w_in, r_in, w_out, r_out, w_buf, r_buf, w_sem, r_sem):
+    width = r_in.shape[1] // PARTS
+
+    def w_copies():
+        return pltpu.make_async_copy(w_in, w_buf, w_sem.at[0]), pltpu.make_async_copy(w_buf, w_out, w_sem.at[1])
+
+    def r_copies(i):
+        at = pl.ds(i * width, width)
+        return (pltpu.make_async_copy(r_in.at[:, at], r_buf.at[i], r_sem.at[0, i]),
+                pltpu.make_async_copy(r_buf.at[i], r_out.at[:, at], r_sem.at[1, i]))
+
+    pairs = [w_copies()] + [r_copies(i) for i in range(PARTS)]
+    for a, _ in pairs:
+        a.start()
+    for a, b in pairs:
+        a.wait()
+        b.start()
+    for _, b in pairs:
+        b.wait()
 
 
 def solution(mesh):
@@ -380,13 +407,25 @@
                 pltpu.VMEM((k, CHUNKS * w2), f32),
                 pltpu.SemaphoreType.DMA((CHUNKS, 32)),
                 pltpu.SemaphoreType.DMA((CHUNKS, 32)),
-                pltpu.SemaphoreType.DMA((CHUNKS, CORES)),
+                pltpu.SemaphoreType.DMA((CHUNKS, CORES, 4)),
                 pltpu.SemaphoreType.DMA,
                 pltpu.SemaphoreType.REGULAR((CHUNKS,)),
             ],
             compiler_params=pltpu.CompilerParams(
                 collective_id=0, has_side_effects=True, vmem_limit_bytes=67043328),
         )(design, targets.T, weights.T, step_sizes[None, :])
+        w_out, r_out = pl.pallas_call(
+            _store,
+            out_shape=(jax.ShapeDtypeStruct((k, feats), f32), jax.ShapeDtypeStruct((k, n), f32)),
+            in_specs=[hb, hb],
+            out_specs=(hb, hb),
+            scratch_shapes=[
+                pltpu.VMEM((k, feats), f32),
+                pltpu.VMEM((PARTS, k, n // PARTS), f32),
+                pltpu.SemaphoreType.DMA((2,)),
+                pltpu.SemaphoreType.DMA((2, PARTS)),
+            ],
+        )(w_out, r_out)
         return w_out.T, r_out.T
 
     return jax.shard_map(

time: 316 us -> 312 us (0.987)
  local copies, waits for them, and re-layouts: 8.11 us -> 0 us
  Pallas kernels: 307 us -> 311 us
    unnamed x2 -> x0, local copies, waits for them, and re-layouts: 8.11 us -> none
    pallas_call x0 -> x1, Pallas kernels: none -> 5.9 us  [local_solve(): pl.pallas_call(_store, out_shape=(jax.ShapeDtypeStruct((k, feats), f32),...]
where the time goes in v5:
time: 312 us
  Pallas kernels  311 us (100%)
    pallas_call x1, Pallas kernels, local_solve(): pl.pallas_call(functools.partial(_kernel, n, side), out_shape=(jax.ShapeD...  305 us

profile of v5, /device:TPU:97, one launch (start us, length us, event | category | flops | bytes accessed | tf_op | source)
XLA Modules:
  0.0 311.8 jit_solution(10805367077531320325)
XLA Ops:
  0.6 305.3 %shard_map.59 = (f32[100,1024]{1,0:T(8,128)}, f32[100,16384]{1,0:T(8,128)}) custom-call(bf16[16384,1024]{1,0:T(8,128)(2,1)} %x_hbm.1, f32[100,16384]{1,0:T(8,128)} %bitcast.5, f32[100,1024]{1,0:T(8,128)} %bitcast.6, f32[1,1024]{1,0:T(1,128)} %bitcast.7), custom_call_target="tpu_custom_call" | custom-call | tf_op jit(solution)/shard_map/pallas_call | solution.py:390
  305.9 5.9 %shard_map.60 = (f32[100,1024]{1,0:T(8,128)}, f32[100,16384]{1,0:T(8,128)}) custom-call(f32[100,1024]{1,0:T(8,128)} %get-tuple-element.6.w_in, f32[100,16384]{1,0:T(8,128)} %get-tuple-element.7.r_in), custom_call_target="tpu_custom_call" | custom-call | tf_op jit(solution)/shard_map/pallas_call | solution.py:417
